TPU v7x, 256 devices: a whole 4x4x8 slice. The times are simulated.
256 devices in a mesh: row: 32 (over y, x, core), col: 8 (over z).
Axes of the slice: x: 4, y: 4, z: 8, core: 2. Of those that a mesh axis runs over, the one named last changes fastest.
Arguments:
- vectors_window: float32 [32, 32, 64, 1024], P(None, 'row', None, 'col'), may hold values from -6 to 6
- column_strip: float32 [32, 32, 64, 1024], P(None, 'row', None, 'col'), may hold values from -6 to 6
- row_strip: float32 [1024, 64, 8, 128], P('row', None, 'col'), may hold values from -6 to 6
- factor: float32 [1024, 1024], P('row', 'col'), may hold values from -2 to 2
- window_start: int32 [1], replicated, may hold values from 1 to 64512
- deflated: int32 [1], replicated, may hold values from 0 to 512
Outputs:
- vectors_updated: float32 [32, 32, 64, 1024], P(None, 'row', None, 'col')
- column_updated: float32 [32, 32, 64, 1024], P(None, 'row', None, 'col')
- row_updated: float32 [1024, 64, 8, 128], P('row', None, 'col')
All inputs are finite; a program needn't handle non-finite values.
Results may differ from a plain program's by a relative error of at most 0.0003.
Values sent between devices are 32-bit elements; how exact they have to be, the bound alone decides.
A program may use at most 64 MiB of HBM per device.

v0:
```python
import jax
import jax.numpy as jnp
from jax import lax
from jax.sharding import PartitionSpec as P

W = 1024


def from_everyone(x, axis):
    peers = lax.axis_size(axis)
    return lax.all_to_all(jnp.broadcast_to(x[None], (peers, *x.shape)), axis, 0, 0, tiled=True)


def laid_out(pieces, dim):
    dims = list(pieces.shape[1:])
    dims[dim] *= pieces.shape[0]
    return jnp.moveaxis(pieces, 0, dim).reshape(dims)


def gather_directly(x, axis, dim):
    pieces = from_everyone(x, axis)
    return laid_out(pieces, dim)


def reflect(factor, deflated):
    columns = jnp.arange(W, dtype=jnp.int32)
    kept_count = W - deflated[0]
    spike_row = jnp.where(columns < kept_count, factor[0], 0.0)
    squares = jnp.sum(spike_row * spike_row)
    corner = factor[0, 0]
    magnitude = jnp.sqrt(squares + 1e-06)
    signum = jnp.where(corner >= 0, 1.0, -1.0)
    vector = spike_row + jnp.where(columns == 0, signum * magnitude, 0.0)
    denominator = squares + 2.0 * jnp.abs(corner) * magnitude + magnitude * magnitude
    scaling = 2.0 / denominator
    reflected_image = jnp.dot(factor, vector, precision=lax.Precision.HIGHEST)
    return factor - scaling * reflected_image[:, None] * vector[None, :]


def body(vectors_window, column_strip, row_strip, factor, window_start, deflated):
    highest = lax.Precision.HIGHEST
    row_position = lax.axis_index("row")
    column_position = lax.axis_index("col")
    start_row = window_start[0]
    widened = gather_directly(factor, "col", 1)
    rotation = reflect(lax.all_gather(widened, "row", axis=0, tiled=True), deflated)
    rounds = vectors_window.shape[0]
    blocks = vectors_window.shape[2]
    local_width = vectors_window.shape[3]
    z_blocks = vectors_window.reshape(rounds, blocks, local_width)
    strip_blocks = column_strip.reshape(rounds, blocks, local_width)
    z_turned = jnp.einsum(
        "rbk,kj->rbj",
        lax.all_to_all(z_blocks, "col", split_axis=1, concat_axis=2, tiled=True),
        rotation,
        precision=highest,
    )
    strip_turned = jnp.einsum(
        "rbk,kj->rbj",
        lax.all_to_all(strip_blocks, "col", split_axis=1, concat_axis=2, tiled=True),
        rotation,
        precision=highest,
    )
    z_rotated = lax.all_to_all(z_turned, "col", split_axis=2, concat_axis=1, tiled=True)
    strip_rotated = lax.all_to_all(strip_turned, "col", split_axis=2, concat_axis=1, tiled=True)
    row_count = lax.axis_size("row")
    round_number = jnp.arange(rounds, dtype=jnp.int32)[:, None]
    block_number = jnp.arange(blocks, dtype=jnp.int32)[None, :]
    row_number = (round_number * row_count + row_position) * blocks + block_number
    column_updated = jnp.where(
        row_number[:, :, None] < start_row, strip_rotated, strip_blocks
    ).reshape(column_strip.shape)
    vectors_updated = z_rotated.reshape(vectors_window.shape)
    strip_rows = row_strip.shape[0]
    flat_strip = row_strip.reshape(strip_rows, -1)
    stacked = lax.all_to_all(flat_strip, "row", split_axis=1, concat_axis=0, tiled=True)
    rotated_rows = lax.dot_general(rotation, stacked, (((0,), (0,)), ((), ())), precision=highest)
    returned = lax.all_to_all(rotated_rows, "row", split_axis=0, concat_axis=1, tiled=True)
    column_count = lax.axis_size("col")
    column_rounds = row_strip.shape[1]
    column_block = row_strip.shape[3]
    round_index = jnp.arange(column_rounds, dtype=jnp.int32)[:, None]
    lane_index = jnp.arange(column_block, dtype=jnp.int32)[None, :]
    column_number = (round_index * column_count + column_position) * column_block + lane_index
    row_updated = jnp.where(
        column_number[None, :, None, :] >= start_row + W,
        returned.reshape(row_strip.shape),
        row_strip,
    )
    return (vectors_updated, column_updated, row_updated)


def solution(mesh):
    return jax.shard_map(
        body,
        mesh=mesh,
        in_specs=(
            P(None, "row", None, "col"),
            P(None, "row", None, "col"),
            P("row", None, "col", None),
            P("row", "col"),
            P(),
            P(),
        ),
        out_specs=(
            P(None, "row", None, "col"),
            P(None, "row", None, "col"),
            P("row", None, "col", None),
        ),
        check_vma=False,
    )
```

profile of v0, /device:TPU:1, one launch (start us, length us, event | category | flops | bytes accessed | tf_op | source)
XLA Modules:
  0.0 231.8 jit_solution(5835078651876137352)
XLA Ops:
  7.2 0.0 all-gather.2.cloned.1.call-start
  7.2 0.7 broadcast_in_dim.44
  7.9 16.6 %all_to_all.106 = f32[8,32,128]{2,1,0:T(8,128)S(1)} all-to-all(f32[8,32,128]{2,1,0:T(8,128)S(1)} %broadcast_in_dim.44), channel_id=1, replica_groups=mesh['row'=32,'col'=8] {'col'}, dimensions={0} | all-to-all | bytes 262144 | tf_op jit(solution)/shard_map/all_to_all | solution.py:11
  24.5 0.7 copy_bitcast_fusion.4
  25.2 0.0 all-gather.2.cloned.1.call-update
  25.2 0.5 broadcast.101
  25.7 4.4 %reduce.3 = f32[32,64,128]{2,1,0:T(8,128)S(1)} reduce(f32[32,64,1,128]{3,2,1,0:T(1,128)} %param.8, f32[]{:T(128)} %broadcast.101), dimensions={2}, to_apply=%param.8.reduce_sub_computation.3 | reduce | bytes 2097156 | tf_op args[2]
  30.2 0.3 all_to_all.93
  30.5 0.0 copy-start.2
  30.5 1.6 copy.61
  32.0 9.4 %all-to-all-start.5 = ((f32[32,32,256]{2,0,1:T(8,128)}), f32[32,32,256]{2,0,1:T(8,128)S(1)}, u32[]{:S(2)}, u32[]{:S(2)}) async-start(f32[32,32,256]{2,0,1:T(8,128)} %copy.61), calls=%async_computation.5 | async-start | bytes 2097152 | tf_op jit(solution)/shard_map/all_to_all | solution.py:76
  41.4 2.8 %copy.74 = f32[32,1,64,128]{3,0,2,1:T(8,128)} copy(f32[32,1,64,128]{3,2,1,0:T(8,128)} %param.6) | data formatting | bytes 2097152 | tf_op args[0]
  44.2 14.1 %all-to-all-done.5 = f32[32,32,256]{2,0,1:T(8,128)S(1)} async-done(((f32[32,32,256]{2,0,1:T(8,128)}), f32[32,32,256]{2,0,1:T(8,128)S(1)}, u32[]{:S(2)}, u32[]{:S(2)}) %all-to-all-start.5) | async-done | bytes 1048608 | tf_op jit(solution)/shard_map/all_to_all | solution.py:76
  58.4 3.6 %all-to-all-start.1 = ((f32[32,64,128]{2,0,1:T(8,128)}), f32[32,64,128]{2,0,1:T(8,128)S(1)}, u32[]{:S(2)}, u32[]{:S(2)}) async-start(f32[32,64,128]{2,0,1:T(8,128)} %bitcast.78), calls=%async_computation.1 | async-start | bytes 2097152 | tf_op jit(solution)/shard_map/all_to_all | solution.py:54
  62.6 0.0 copy-done.2
  62.7 1.6 copy.72
  64.2 16.0 %all-gather.2.cloned.1.call-done = f32[1024,1024]{1,0:T(8,128)} async-done(((f32[32,1024]{1,0:T(8,128)}), f32[1024,1024]{1,0:T(8,128)}) %all-gather.2.cloned.1.call-update) | async-done | bytes 4194320 | tf_op jit(solution)/shard_map/all_gather | solution.py:46
  80.3 0.8 slice.8
  81.0 10.2 %all-to-all-done.1 = f32[32,64,128]{2,0,1:T(8,128)S(1)} async-done(((f32[32,64,128]{2,0,1:T(8,128)}), f32[32,64,128]{2,0,1:T(8,128)S(1)}, u32[]{:S(2)}, u32[]{:S(2)}) %all-to-all-start.1) | async-done | bytes 1048608 | tf_op jit(solution)/shard_map/all_to_all | solution.py:54
  91.2 3.7 %all-to-all-start.3 = ((f32[32,64,128]{2,0,1:T(8,128)}), f32[32,64,128]{2,0,1:T(8,128)S(1)}, u32[]{:S(2)}, u32[]{:S(2)}) async-start(f32[32,64,128]{2,0,1:T(8,128)} %bitcast.76), calls=%async_computation.3 | async-start | bytes 2097152 | tf_op jit(solution)/shard_map/all_to_all | solution.py:60
  94.9 0.6 multiply_reduce_fusion
  95.5 1.2 slice.9
  99.4 0.0 copy-start
  99.4 5.8 %fusion.17 = f32[1,1024]{1,0:T(1,128)S(1)} fusion(f32[1024,1]{0,1:T(1,128)S(1)} %bitcast.101, f32[1024,1024]{1,0:T(8,128)} %all-gather.2.cloned.1.call-done), kind=kOutput, calls=%fused_computation.32 | convolution fusion | flops 12582912 | bytes 4202496 | tf_op jit(solution)/shard_map/dot_general | solution.py:36
  105.2 0.0 copy-done
  105.3 2.4 %fusion.4 = f32[1024,1024]{0,1:T(8,128)} fusion(f32[1024,1024]{1,0:T(8,128)S(1)} %copy-done, f32[1024]{0:T(1024)S(1)} %bitcast.97, f32[1024]{0:T(1024)S(1)} %broadcast_multiply_fusion), kind=kLoop, calls=%fused_computation.5 | loop fusion | flops 2097152 | bytes 8396800 | tf_op jit(solution)/shard_map/dot_general | solution.py:77
  107.6 5.4 %copy.60 = f32[1024,1024]{1,0:T(8,128)} copy(f32[1024,1024]{0,1:T(8,128)} %fusion.4) | data formatting | bytes 8388608 | tf_op jit(solution)/shard_map/dot_general | solution.py:77
  113.0 6.6 %fusion.18 = f32[32,32,256]{2,1,0:T(8,128)} fusion(f32[32,32,1024]{2,1,0:T(8,128)} %bitcast.85, f32[1024,256,1]{1,0,2:T(8,128)S(1)} %bitcast.92), kind=kOutput, calls=%fused_computation.33 | convolution fusion | flops 3221225472 | bytes 6291456 | tf_op jit(solution)/shard_map/dot_general | solution.py:77
  119.6 2.3 %all-to-all-done.3 = f32[32,64,128]{2,0,1:T(8,128)S(1)} async-done(((f32[32,64,128]{2,0,1:T(8,128)}), f32[32,64,128]{2,0,1:T(8,128)S(1)}, u32[]{:S(2)}, u32[]{:S(2)}) %all-to-all-start.3) | async-done | bytes 1048608 | tf_op jit(solution)/shard_map/all_to_all | solution.py:60
  121.9 5.0 %all-to-all-start.6 = ((f32[32,32,256]{2,1,0:T(8,128)}), f32[32,32,256]{2,1,0:T(8,128)S(1)}, u32[]{:S(2)}, u32[]{:S(2)}) async-start(f32[32,32,256]{2,1,0:T(8,128)} %fusion.18), calls=%async_computation.6 | async-start | bytes 2097152 | tf_op jit(solution)/shard_map/all_to_all | solution.py:78
  126.9 1.6 copy.73
  128.5 2.4 %all_to_all.81 = f32[32,8,1024]{2,0,1:T(8,128)} reshape(f32[32,8,8,128]{3,2,0,1:T(8,128)} %bitcast.90) | data formatting | bytes 2097152 | tf_op jit(solution)/shard_map/all_to_all | solution.py:54
  130.8 6.4 %fusion.9 = f32[32,8,1024]{2,0,1:T(8,128)S(1)} fusion(f32[32,8,1024]{2,0,1:T(8,128)} %all_to_all.81, f32[1024,1024]{1,0:T(8,128)} %all-gather.2.cloned.1.call-done, f32[1024]{0:T(1024)S(1)} %bitcast.98, f32[1024]{0:T(1024)S(1)} %broadcast_multiply_fusion), kind=kOutput, calls=%fused_computation.10 | convolution fusion | flops 3223322624 | bytes 6299648 | tf_op jit(solution)/shard_map/rbk,kj->rbj/dot_general | solution.py:52
  137.2 2.7 %copy.54 = f32[32,8,1024]{0,1,2:T(8,128)} copy(f32[32,8,1024]{2,0,1:T(8,128)S(1)} %fusion.9) | data formatting | bytes 2097152 | tf_op jit(solution)/shard_map/rbk,kj->rbj/dot_general | solution.py:52
  140.0 4.8 %reshape.143 = f32[8,1,32768]{2,1,0:T(1,128)} reshape(f32[1024,8,32]{2,1,0:T(8,128)} %bitcast.81) | data formatting | bytes 2097152
  144.8 0.0 all-to-all-done.6
  144.8 0.0 copy-start.4
  144.8 1.0 copy-done.4
  145.8 4.3 %all-to-all-start.2 = ((f32[8,1,32768]{2,1,0:T(1,128)}), f32[8,1,32768]{2,1,0:T(1,128)S(1)}, u32[]{:S(2)}, u32[]{:S(2)}) async-start(f32[8,1,32768]{2,1,0:T(1,128)} %reshape.143), calls=%async_computation.2 | async-start | bytes 2097152 | tf_op jit(solution)/shard_map/all_to_all | solution.py:64
  150.1 0.6 copy.71
  150.7 1.1 all_to_all.88
  151.8 6.4 %fusion.12 = f32[32,8,1024]{2,0,1:T(8,128)S(1)} fusion(f32[32,8,1024]{2,0,1:T(8,128)} %all_to_all.88, f32[1024,1024]{1,0:T(8,128)} %all-gather.2.cloned.1.call-done, f32[1024]{0:T(1024)S(1)} %bitcast.99, f32[1024]{0:T(1024)S(1)} %broadcast_multiply_fusion), kind=kOutput, calls=%fused_computation.11 | convolution fusion | flops 3223322624 | bytes 6299648 | tf_op jit(solution)/shard_map/rbk,kj->rbj/dot_general | solution.py:58
  158.2 2.7 %copy.58 = f32[32,8,1024]{0,1,2:T(8,128)} copy(f32[32,8,1024]{2,0,1:T(8,128)S(1)} %fusion.12) | data formatting | bytes 2097152 | tf_op jit(solution)/shard_map/rbk,kj->rbj/dot_general | solution.py:58
  160.9 4.9 %reshape.145 = f32[8,1,32768]{2,1,0:T(1,128)} reshape(f32[1024,8,32]{2,1,0:T(8,128)} %bitcast.82) | data formatting | bytes 2097152
  165.9 13.5 %all-to-all-done.2 = f32[8,1,32768]{2,1,0:T(1,128)S(1)} async-done(((f32[8,1,32768]{2,1,0:T(1,128)}), f32[8,1,32768]{2,1,0:T(1,128)S(1)}, u32[]{:S(2)}, u32[]{:S(2)}) %all-to-all-start.2) | async-done | bytes 1048608 | tf_op jit(solution)/shard_map/all_to_all | solution.py:64
  179.3 4.2 %all-to-all-start.4 = ((f32[8,1,32768]{2,1,0:T(1,128)}), f32[8,1,32768]{2,1,0:T(1,128)}, u32[]{:S(2)}, u32[]{:S(2)}) async-start(f32[8,1,32768]{2,1,0:T(1,128)} %reshape.145), calls=%async_computation.4 | async-start | bytes 2097152 | tf_op jit(solution)/shard_map/all_to_all | solution.py:65
  184.3 0.1 add_compare_fusion.1
  184.3 0.1 add_compare_fusion
  184.4 0.0 copy-done.5
  184.4 1.6 copy.62
  186.0 1.3 reshape.129
  187.3 0.0 copy-done.1
  187.3 1.1 broadcast_select_fusion
  188.4 0.5 broadcast.102
  189.0 3.1 %reduce.4 = f32[8,32768]{1,0:T(8,128)S(1)} reduce(f32[8,1,32768]{2,1,0:T(1,128)S(1)} %all-to-all-done.2, f32[]{:T(128)} %broadcast.102), dimensions={1}, to_apply=%all_to_all.82.reduce_sub_computation | reduce | bytes 2097156 | tf_op jit(solution)/shard_map/all_to_all | solution.py:64
  192.0 3.3 %reshape.144 = f32[1024,8,32]{2,1,0:T(8,128)} reshape(f32[8,32768]{1,0:T(8,128)S(1)} %reduce.4) | data formatting | bytes 2097152
  195.3 3.9 %copy.55 = f32[32,8,8,128]{3,2,1,0:T(8,128)} copy(f32[32,8,8,128]{0,2,3,1:T(8,128)} %bitcast.83) | data formatting | bytes 2097152 | tf_op jit(solution)/shard_map/all_to_all | solution.py:64
  199.3 13.5 %all-to-all-done.4 = f32[8,1,32768]{2,1,0:T(1,128)} async-done(((f32[8,1,32768]{2,1,0:T(1,128)}), f32[8,1,32768]{2,1,0:T(1,128)}, u32[]{:S(2)}, u32[]{:S(2)}) %all-to-all-start.4) | async-done | bytes 1048608 | tf_op jit(solution)/shard_map/all_to_all | solution.py:65
  212.8 4.3 %reduce.5 = f32[8,32768]{1,0:T(8,128)S(1)} reduce(f32[8,1,32768]{2,1,0:T(1,128)} %all-to-all-done.4, f32[]{:T(128)} %broadcast.102), dimensions={1}, to_apply=%all_to_all.89.reduce_sub_computation | reduce | bytes 2097156 | tf_op jit(solution)/shard_map/all_to_all | solution.py:65
  217.1 0.0 copy-start.3
  217.1 3.3 %reshape.146 = f32[1024,8,32]{2,1,0:T(8,128)} reshape(f32[8,32768]{1,0:T(8,128)S(1)} %reduce.5) | data formatting | bytes 2097152
  220.4 3.2 %copy.59 = f32[32,8,8,128]{3,2,1,0:T(8,128)S(1)} copy(f32[32,8,8,128]{0,2,3,1:T(8,128)} %bitcast.84) | data formatting | bytes 2097152 | tf_op jit(solution)/shard_map/all_to_all | solution.py:65
  223.6 0.0 copy-done.3
  223.7 1.3 bitcast_select_fusion
  (7 shorter events, 0.0 us)
Async XLA Ops:
  7.2 73.1 %all-gather.2.cloned.1.call-start = ((), (), s32[]{:S(2)}) async-start(), calls=%async_computation.7 | async-start | bytes 4325376 | tf_op jit(solution)/shard_map/all_gather | solution.py:46
  30.5 32.2 %copy-start.2 = (f32[32,1,64,128]{3,2,1,0:T(8,128)S(1)}, f32[32,1,64,128]{3,2,1,0:T(8,128)}, u32[]{:S(2)}) copy-start(f32[32,1,64,128]{3,2,1,0:T(8,128)} %param.7) | copy-start | bytes 3145732
  32.0 26.3 %all-to-all-start.5 = ((f32[32,32,256]{2,0,1:T(8,128)}), f32[32,32,256]{2,0,1:T(8,128)S(1)}, u32[]{:S(2)}, u32[]{:S(2)}) async-start(f32[32,32,256]{2,0,1:T(8,128)} %copy.61), calls=%async_computation.5 | async-start | bytes 2097152 | tf_op jit(solution)/shard_map/all_to_all | solution.py:76
  58.4 32.8 %all-to-all-start.1 = ((f32[32,64,128]{2,0,1:T(8,128)}), f32[32,64,128]{2,0,1:T(8,128)S(1)}, u32[]{:S(2)}, u32[]{:S(2)}) async-start(f32[32,64,128]{2,0,1:T(8,128)} %bitcast.78), calls=%async_computation.1 | async-start | bytes 2097152 | tf_op jit(solution)/shard_map/all_to_all | solution.py:54
  91.2 30.7 %all-to-all-start.3 = ((f32[32,64,128]{2,0,1:T(8,128)}), f32[32,64,128]{2,0,1:T(8,128)S(1)}, u32[]{:S(2)}, u32[]{:S(2)}) async-start(f32[32,64,128]{2,0,1:T(8,128)} %bitcast.76), calls=%async_computation.3 | async-start | bytes 2097152 | tf_op jit(solution)/shard_map/all_to_all | solution.py:60
  99.4 5.8 %copy-start = (f32[1024,1024]{1,0:T(8,128)S(1)}, f32[1024,1024]{1,0:T(8,128)}, u32[]{:S(2)}) copy-start(f32[1024,1024]{1,0:T(8,128)} %all-gather.2.cloned.1.call-done) | copy-start | bytes 12582916
  121.9 22.9 %all-to-all-start.6 = ((f32[32,32,256]{2,1,0:T(8,128)}), f32[32,32,256]{2,1,0:T(8,128)S(1)}, u32[]{:S(2)}, u32[]{:S(2)}) async-start(f32[32,32,256]{2,1,0:T(8,128)} %fusion.18), calls=%async_computation.6 | async-start | bytes 2097152 | tf_op jit(solution)/shard_map/all_to_all | solution.py:78
  144.8 1.0 copy-start.4
  145.8 33.6 %all-to-all-start.2 = ((f32[8,1,32768]{2,1,0:T(1,128)}), f32[8,1,32768]{2,1,0:T(1,128)S(1)}, u32[]{:S(2)}, u32[]{:S(2)}) async-start(f32[8,1,32768]{2,1,0:T(1,128)} %reshape.143), calls=%async_computation.2 | async-start | bytes 2097152 | tf_op jit(solution)/shard_map/all_to_all | solution.py:64
  160.9 23.5 %copy-start.5 = (f32[32,32,256]{2,1,0:T(8,128)S(1)}, f32[32,32,256]{2,1,0:T(8,128)}, u32[]{:S(2)}) copy-start(f32[32,32,256]{2,1,0:T(8,128)} %copy-done.4) | copy-start | bytes 3145732
  165.9 21.5 %copy-start.1 = (f32[32,64,1,128]{3,2,1,0:T(1,128)S(1)}, f32[32,64,1,128]{3,2,1,0:T(1,128)}, u32[]{:S(2)}) copy-start(f32[32,64,1,128]{3,2,1,0:T(1,128)} %param.8) | copy-start | bytes 3145732
  179.3 33.5 %all-to-all-start.4 = ((f32[8,1,32768]{2,1,0:T(1,128)}), f32[8,1,32768]{2,1,0:T(1,128)}, u32[]{:S(2)}, u32[]{:S(2)}) async-start(f32[8,1,32768]{2,1,0:T(1,128)} %reshape.145), calls=%async_computation.4 | async-start | bytes 2097152 | tf_op jit(solution)/shard_map/all_to_all | solution.py:65
  217.1 6.5 %copy-start.3 = (f32[32,1,64,128]{3,2,1,0:T(8,128)S(1)}, f32[32,1,64,128]{3,2,1,0:T(8,128)}, u32[]{:S(2)}) copy-start(f32[32,1,64,128]{3,2,1,0:T(8,128)} %param.7) | copy-start | bytes 3145732
Sparse Core Ops, SparseCore 0:
  25.3 54.9 all-gather.1
where the time goes:
time: 233 us; the launch traced here: 232 us
  waiting for transfers between devices  69.7 us (30%)
  local copies, waits for them, and re-layouts  54.5 us (23%)
  starting transfers between devices  30.3 us (13%)
  matrix products  25.2 us (11%)
  between operations  18.2 us (8%)
  other arithmetic  17.4 us (7%)
  blocking collectives  16.6 us (7%)
    unnamed x19, local copies, waits for them, and re-layouts  22.3 us
    all_to_all x1, blocking collectives, from_everyone(): lax.all_to_all(jnp.broadcast_to(x[None], (peers, *x.shape)), axis, 0, 0,...  16.6 us
    all_gather x1, waiting for transfers between devices, body(): lax.all_gather(widened, 'row', axis=0, tiled=True)  16 us
    all_to_all x1, waiting for transfers between devices, body(): lax.all_to_all(flat_strip, 'row', split_axis=1, concat_axis=0, tiled=True)  14.1 us
    all_to_all x1, waiting for transfers between devices, body(): lax.all_to_all(strip_turned, 'col', split_axis=2, concat_axis=1, tiled=True)  13.5 us
    all_to_all x1, waiting for transfers between devices, body(): lax.all_to_all(z_turned, 'col', split_axis=2, concat_axis=1, tiled=True)  13.5 us
    all_to_all x1, waiting for transfers between devices, body(): lax.all_to_all(z_blocks, 'col', split_axis=1, concat_axis=2, tiled=True)  10.2 us
    all_to_all x1, starting transfers between devices, body(): lax.all_to_all(flat_strip, 'row', split_axis=1, concat_axis=0, tiled=True)  9.38 us
  transfers between devices with their start and end apart: 7, of which 6 were waited for; matrix products, arithmetic and copies ran while one was open for 34% of the time, Pallas kernels for 0%

commit v1 on v0

--- a/solution.py
+++ b/solution.py
@@ -61,7 +61,18 @@
         rotation,
         precision=highest,
     )
-    z_rotated = lax.all_to_all(z_turned, "col", split_axis=2, concat_axis=1, tiled=True)
+    ways, here = (lax.axis_size("col"), lax.axis_index("col"))
+    width = z_turned.shape[2] // ways
+    shape = list(z_turned.shape)
+    shape[2] = width
+    height = shape[1]
+    shape[1] = height * ways
+    z_rotated = jnp.zeros(shape, z_turned.dtype)
+    for mask in range(ways):
+        part = lax.dynamic_slice_in_dim(z_turned, (here ^ mask) * width, width, axis=2)
+        if mask:
+            part = lax.ppermute(part, "col", [(d, d ^ mask) for d in range(ways)])
+        z_rotated = lax.dynamic_update_slice_in_dim(z_rotated, part, (here ^ mask) * height, axis=1)
     strip_rotated = lax.all_to_all(strip_turned, "col", split_axis=2, concat_axis=1, tiled=True)
     row_count = lax.axis_size("row")
     round_number = jnp.arange(rounds, dtype=jnp.int32)[:, None]

time: 233 us -> 232 us (level)
  starting transfers between devices: 30.3 us -> 37.8 us
  waiting for transfers between devices: 69.7 us -> 66.3 us
    ppermute x0 -> x7, waiting for transfers between devices: none -> 22.6 us  [body(): part = lax.ppermute(part, 'col', [(d, d ^ mask) for d in range(ways)])]
    all_to_all x1, waiting for transfers between devices: 10.2 us -> 27.4 us  [body(): lax.all_to_all(z_blocks, 'col', split_axis=1, concat_axis=2, tiled=True)]
    all_gather x1, waiting for transfers between devices: 16 us -> 0.01 us  [body(): lax.all_gather(widened, 'row', axis=0, tiled=True)]
    all_to_all x1, waiting for transfers between devices: 14.1 us -> 0.01 us  [body(): lax.all_to_all(flat_strip, 'row', split_axis=1, concat_axis=0, tiled=True)]
    all_to_all x1, waiting for transfers between devices: 2.34 us -> 16.2 us  [body(): lax.all_to_all(strip_blocks, 'col', split_axis=1, concat_axis=2, tiled=True)]
    all_to_all x1, waiting for transfers between devices: 13.5 us -> 0.01 us  [body(): lax.all_to_all(strip_turned, 'col', split_axis=2, concat_axis=1, tiled=True)]
    all_to_all x1 -> x0, waiting for transfers between devices: 13.5 us -> none  [body(): lax.all_to_all(z_turned, 'col', split_axis=2, concat_axis=1, tiled=True)]
    ppermute x0 -> x7, starting transfers between devices: none -> 10.5 us  [body(): part = lax.ppermute(part, 'col', [(d, d ^ mask) for d in range(ways)])]
  transfers between devices with their start and end apart: 7 -> 13, of which waited for: 6 -> 3; matrix products, arithmetic and copies ran while one was open for 34% -> 29% of each run, Pallas kernels for 0% -> 0%
where the time goes in v1:
time: 232 us; the launch traced here: 231 us
  waiting for transfers between devices  66.3 us (29%)
  local copies, waits for them, and re-layouts  52.8 us (23%)
  starting transfers between devices  37.8 us (16%)
  matrix products  23.3 us (10%)
  between operations  18.4 us (8%)
  blocking collectives  16.6 us (7%)
  other arithmetic  15.5 us (7%)
    all_to_all x1, waiting for transfers between devices, body(): lax.all_to_all(z_blocks, 'col', split_axis=1, concat_axis=2, tiled=True)  27.4 us
    ppermute x7, waiting for transfers between devices, body(): part = lax.ppermute(part, 'col', [(d, d ^ mask) for d in range(ways)])  22.6 us
    all_to_all x1, blocking collectives, from_everyone(): lax.all_to_all(jnp.broadcast_to(x[None], (peers, *x.shape)), axis, 0, 0,...  16.6 us
    all_to_all x1, waiting for transfers between devices, body(): lax.all_to_all(strip_blocks, 'col', split_axis=1, concat_axis=2, tiled=True)  16.2 us
    unnamed x23, local copies, waits for them, and re-layouts  15.1 us
    ppermute x7, starting transfers between devices, body(): part = lax.ppermute(part, 'col', [(d, d ^ mask) for d in range(ways)])  10.5 us
    dynamic_update_slice x8, local copies, waits for them, and re-layouts, body(): lax.dynamic_update_slice_in_dim(z_rotated, part, (here ^ mask) * height,...  9.75 us
    all_to_all x1, starting transfers between devices, body(): lax.all_to_all(flat_strip, 'row', split_axis=1, concat_axis=0, tiled=True)  7.68 us
  transfers between devices with their start and end apart: 13, of which 3 were waited for; matrix products, arithmetic and copies ran while one was open for 29% of the time, Pallas kernels for 0%

profile of v1, /device:TPU:1, one launch (start us, length us, event | category | flops | bytes accessed | tf_op | source)
XLA Modules:
  0.0 230.7 jit_solution(10410297355325712757)
XLA Ops:
  7.2 0.0 all-gather.2.cloned.1.call-start
  7.2 0.8 broadcast_in_dim.45
  8.0 16.6 %all_to_all.91 = f32[8,32,128]{2,1,0:T(8,128)S(1)} all-to-all(f32[8,32,128]{2,1,0:T(8,128)S(1)} %broadcast_in_dim.45), channel_id=1, replica_groups=mesh['row'=32,'col'=8] {'col'}, dimensions={0} | all-to-all | bytes 262144 | tf_op jit(solution)/shard_map/all_to_all | solution.py:11
  24.6 0.7 copy_bitcast_fusion.4
  25.2 0.0 all-gather.2.cloned.1.call-update
  25.3 0.0 copy-start.1
  25.3 2.9 %copy.114 = f32[32,1,64,128]{3,0,2,1:T(8,128)} copy(f32[32,1,64,128]{3,2,1,0:T(8,128)} %param.6) | data formatting | bytes 2097152 | tf_op args[0]
  28.2 3.6 %all-to-all-start.1 = ((f32[32,64,128]{2,0,1:T(8,128)}), f32[32,64,128]{2,0,1:T(8,128)S(1)}, u32[]{:S(2)}, u32[]{:S(2)}) async-start(f32[32,64,128]{2,0,1:T(8,128)} %bitcast.104), calls=%async_computation.1 | async-start | bytes 2097152 | tf_op jit(solution)/shard_map/all_to_all | solution.py:54
  31.8 1.6 copy.112
  33.3 27.4 %all-to-all-done.1 = f32[32,64,128]{2,0,1:T(8,128)S(1)} async-done(((f32[32,64,128]{2,0,1:T(8,128)}), f32[32,64,128]{2,0,1:T(8,128)S(1)}, u32[]{:S(2)}, u32[]{:S(2)}) %all-to-all-start.1) | async-done | bytes 1048608 | tf_op jit(solution)/shard_map/all_to_all | solution.py:54
  60.8 1.0 copy-done.4
  61.7 3.6 %all-to-all-start.2 = ((f32[32,64,128]{2,0,1:T(8,128)}), f32[32,64,128]{2,0,1:T(8,128)S(1)}, u32[]{:S(2)}, u32[]{:S(2)}) async-start(f32[32,64,128]{2,0,1:T(8,128)} %bitcast.102), calls=%async_computation.2 | async-start | bytes 2097152 | tf_op jit(solution)/shard_map/all_to_all | solution.py:60
  66.7 0.5 broadcast.103
  67.2 3.2 %reduce.3 = f32[32,64,128]{2,1,0:T(8,128)S(1)} reduce(f32[32,64,1,128]{3,2,1,0:T(1,128)S(1)} %copy-done.1, f32[]{:T(128)} %broadcast.103), dimensions={2}, to_apply=%param.8.reduce_sub_computation.3 | reduce | bytes 2097156 | tf_op args[2]
  70.4 1.3 all_to_all.79
  71.7 2.9 %copy.93 = f32[32,32,256]{2,0,1:T(8,128)} copy(f32[32,32,256]{2,1,0:T(8,128)} %all_to_all.79) | data formatting | bytes 2097152 | tf_op jit(solution)/shard_map/all_to_all | solution.py:87
  74.6 0.7 add_compare_fusion.1
  75.2 0.1 add_compare_fusion
  75.3 1.8 copy.113
  77.1 1.1 all_to_all.70
  78.3 16.2 %all-to-all-done.2 = f32[32,64,128]{2,0,1:T(8,128)S(1)} async-done(((f32[32,64,128]{2,0,1:T(8,128)}), f32[32,64,128]{2,0,1:T(8,128)S(1)}, u32[]{:S(2)}, u32[]{:S(2)}) %all-to-all-start.2) | async-done | bytes 1048608 | tf_op jit(solution)/shard_map/all_to_all | solution.py:60
  94.5 7.7 %all-to-all-start.4 = ((f32[32,32,256]{2,0,1:T(8,128)}), f32[32,32,256]{2,0,1:T(8,128)}, u32[]{:S(2)}, u32[]{:S(2)}) async-start(f32[32,32,256]{2,0,1:T(8,128)} %copy.93), calls=%async_computation.4 | async-start | bytes 2097152 | tf_op jit(solution)/shard_map/all_to_all | solution.py:87
  102.1 0.6 copy.111
  102.8 1.1 all_to_all.74
  103.9 0.8 slice.8
  104.6 0.7 multiply_reduce_fusion
  106.0 1.2 slice.9
  107.9 5.6 %fusion.14 = f32[1,1024]{1,0:T(1,128)S(1)} fusion(f32[1024,1]{0,1:T(1,128)S(1)} %bitcast.116, f32[1024,1024]{1,0:T(8,128)} %all-gather.2.cloned.1.call-done), kind=kOutput, calls=%fused_computation.47 | convolution fusion | flops 12582912 | bytes 4202496 | tf_op jit(solution)/shard_map/dot_general | solution.py:36
  114.9 0.8 fusion.12
  115.7 4.6 %fusion.4 = f32[1024,1024]{0,1:T(8,128)} fusion(f32[1024,1024]{1,0:T(8,128)} %all-gather.2.cloned.1.call-done, f32[1024]{0:T(1024)S(1)} %bitcast.112, f32[1024]{0:T(1024)S(1)} %broadcast_multiply_fusion), kind=kLoop, calls=%fused_computation.5 | loop fusion | flops 2097152 | bytes 8396800 | tf_op jit(solution)/shard_map/dot_general | solution.py:88
  120.3 5.4 %copy.92 = f32[1024,1024]{1,0:T(8,128)} copy(f32[1024,1024]{0,1:T(8,128)} %fusion.4) | data formatting | bytes 8388608 | tf_op jit(solution)/shard_map/dot_general | solution.py:88
  125.7 7.1 %fusion.15 = f32[32,32,256]{2,1,0:T(8,128)} fusion(f32[32,32,1024]{2,1,0:T(8,128)} %bitcast.98, f32[1024,256,1]{1,0,2:T(8,128)} %bitcast.40), kind=kOutput, calls=%fused_computation.48 | convolution fusion | flops 3221225472 | bytes 6291456 | tf_op jit(solution)/shard_map/dot_general | solution.py:88
  132.8 7.4 %all-to-all-start.5 = ((f32[32,32,256]{2,1,0:T(8,128)}), f32[32,32,256]{2,1,0:T(8,128)S(1)}, u32[]{:S(2)}, u32[]{:S(2)}) async-start(f32[32,32,256]{2,1,0:T(8,128)} %fusion.15), calls=%async_computation.5 | async-start | bytes 2097152 | tf_op jit(solution)/shard_map/all_to_all | solution.py:89
  140.2 6.3 %fusion.2 = f32[1024,32,8]{0,1,2:T(8,128)S(1)} fusion(f32[32,8,1024]{2,0,1:T(8,128)S(1)} %copy-done.6, f32[1024,1024]{1,0:T(8,128)} %all-gather.2.cloned.1.call-done, f32[1024]{0:T(1024)S(1)} %bitcast.113, f32[1024]{0:T(1024)S(1)} %broadcast_multiply_fusion), kind=kOutput, calls=%fused_computation.2 | convolution fusion | flops 3223322624 | bytes 6299648 | tf_op jit(solution)/shard_map/rbk,kj->rbj/dot_general | solution.py:52
  146.5 0.9 dynamic-slice_bitcast_fusion
  147.4 0.3 collective-permute-start
  147.6 3.3 %collective-permute-start.2 = (f32[32,8,128]{2,0,1:T(8,128)}, f32[32,8,128]{2,0,1:T(8,128)}, u32[]{:S(2)}, u32[]{:S(2)}) collective-permute-start(f32[32,8,128]{2,0,1:T(8,128)} %get-tuple-element.19), channel_id=1, source_target_pairs={{0,3},{1,2},{2,1},{3,0},{4,7},{5,6},{6,5},{7,4},{8,11},{9,10},{10,... | collective-permute-start | bytes 393224 | tf_op jit(solution)/shard_map/ppermute | solution.py:74
  150.9 0.2 collective-permute-start.3
  151.2 3.3 %collective-permute-start.4 = (f32[32,8,128]{2,0,1:T(8,128)}, f32[32,8,128]{2,0,1:T(8,128)}, u32[]{:S(2)}, u32[]{:S(2)}) collective-permute-start(f32[32,8,128]{2,0,1:T(8,128)} %get-tuple-element.17), channel_id=1, source_target_pairs={{0,5},{1,4},{2,7},{3,6},{4,1},{5,0},{6,3},{7,2},{8,13},{9,12},{10,... | collective-permute-start | bytes 393224 | tf_op jit(solution)/shard_map/ppermute | solution.py:74
  154.5 4.3 %fusion.9 = f32[32,8,1024]{2,0,1:T(8,128)S(1)} fusion(f32[32,8,1024]{2,0,1:T(8,128)S(1)} %copy-done.5, f32[1024,1024]{1,0:T(8,128)S(1)} %copy-done, f32[1024]{0:T(1024)S(1)} %bitcast.114, f32[1024]{0:T(1024)S(1)} %broadcast_multiply_fusion), kind=kOutput, calls=%fused_computation.10 | convolution fusion | flops 3223322624 | bytes 6299648 | tf_op jit(solution)/shard_map/rbk,kj->rbj/dot_general | solution.py:58
  158.8 2.7 %copy.90 = f32[32,8,1024]{0,1,2:T(8,128)} copy(f32[32,8,1024]{2,0,1:T(8,128)S(1)} %fusion.9) | data formatting | bytes 2097152 | tf_op jit(solution)/shard_map/rbk,kj->rbj/dot_general | solution.py:58
  161.5 4.8 %reshape.182 = f32[8,1,32768]{2,1,0:T(1,128)} reshape(f32[1024,8,32]{2,1,0:T(8,128)} %bitcast.96) | data formatting | bytes 2097152
  166.3 0.1 reshape.156
  166.4 0.1 copy_dynamic-update-slice_fusion.7
  166.5 0.9 copy-done.7
  167.5 0.8 collective-permute-start.5
  168.3 5.0 %all-to-all-start.3 = ((f32[8,1,32768]{2,1,0:T(1,128)}), f32[8,1,32768]{2,1,0:T(1,128)S(1)}, u32[]{:S(2)}, u32[]{:S(2)}) async-start(f32[8,1,32768]{2,1,0:T(1,128)} %reshape.182), calls=%async_computation.3 | async-start | bytes 2097152 | tf_op jit(solution)/shard_map/all_to_all | solution.py:76
  173.3 1.6 copy_dynamic-update-slice_fusion.6
  174.9 2.7 %collective-permute-start.6 = (f32[32,8,128]{2,0,1:T(8,128)S(1)}, f32[32,8,128]{2,0,1:T(8,128)S(1)}, u32[]{:S(2)}, u32[]{:S(2)}) collective-permute-start(f32[32,8,128]{2,0,1:T(8,128)S(1)} %get-tuple-element.15), channel_id=1, source_target_pairs={{0,7},{1,6},{2,5},{3,4},{4,3},{5,2},{6,1},{7,0},{8,15},{9,14},{10,... | collective-permute-start | bytes 393224 | tf_op jit(solution)/shard_map/ppermute | solution.py:74
  177.6 1.6 copy_dynamic-update-slice_fusion.5
  179.2 1.6 copy_dynamic-update-slice_fusion.4
  180.9 1.6 copy_dynamic-update-slice_fusion.3
  182.5 1.6 copy_dynamic-update-slice_fusion.2
  184.2 0.7 copy_dynamic-update-slice_fusion.1
  184.9 22.6 %collective-permute-done.6 = f32[32,8,128]{2,0,1:T(8,128)S(1)} collective-permute-done((f32[32,8,128]{2,0,1:T(8,128)S(1)}, f32[32,8,128]{2,0,1:T(8,128)S(1)}, u32[]{:S(2)}, u32[]{:S(2)}) %collective-permute-start.6) | collective-permute-done | bytes 131104 | tf_op jit(solution)/shard_map/ppermute | solution.py:74
  207.5 0.7 copy_dynamic-update-slice_fusion
  208.3 1.6 copy.94
  209.9 1.3 reshape.168
  211.1 1.1 broadcast_select_fusion
  212.3 0.5 broadcast.104
  212.8 3.1 %reduce.4 = f32[8,32768]{1,0:T(8,128)S(1)} reduce(f32[8,1,32768]{2,1,0:T(1,128)S(1)} %all-to-all-done.3, f32[]{:T(128)} %broadcast.104), dimensions={1}, to_apply=%all_to_all.75.reduce_sub_computation | reduce | bytes 2097156 | tf_op jit(solution)/shard_map/all_to_all | solution.py:76
  215.9 3.3 %reshape.183 = f32[1024,8,32]{2,1,0:T(8,128)} reshape(f32[8,32768]{1,0:T(8,128)S(1)} %reduce.4) | data formatting | bytes 2097152
  219.3 3.2 %copy.91 = f32[32,8,8,128]{3,2,1,0:T(8,128)S(1)} copy(f32[32,8,8,128]{0,2,3,1:T(8,128)} %bitcast.97) | data formatting | bytes 2097152 | tf_op jit(solution)/shard_map/all_to_all | solution.py:76
  222.5 1.3 bitcast_select_fusion
  (30 shorter events, 0.1 us)
Async XLA Ops:
  7.2 24.6 %copy-start.2 = (f32[32,1,64,128]{3,2,1,0:T(8,128)S(1)}, f32[32,1,64,128]{3,2,1,0:T(8,128)}, u32[]{:S(2)}) copy-start(f32[32,1,64,128]{3,2,1,0:T(8,128)} %param.7) | copy-start | bytes 3145732
  7.2 96.7 %all-gather.2.cloned.1.call-start = ((), (), s32[]{:S(2)}) async-start(), calls=%async_computation.6 | async-start | bytes 4325376 | tf_op jit(solution)/shard_map/all_gather | solution.py:46
  25.3 41.9 %copy-start.1 = (f32[32,64,1,128]{3,2,1,0:T(1,128)S(1)}, f32[32,64,1,128]{3,2,1,0:T(1,128)}, u32[]{:S(2)}) copy-start(f32[32,64,1,128]{3,2,1,0:T(1,128)} %param.8) | copy-start | bytes 3145732
  28.2 32.6 %all-to-all-start.1 = ((f32[32,64,128]{2,0,1:T(8,128)}), f32[32,64,128]{2,0,1:T(8,128)S(1)}, u32[]{:S(2)}, u32[]{:S(2)}) async-start(f32[32,64,128]{2,0,1:T(8,128)} %bitcast.104), calls=%async_computation.1 | async-start | bytes 2097152 | tf_op jit(solution)/shard_map/all_to_all | solution.py:54
  60.8 1.0 copy-start.4
  61.7 32.7 %all-to-all-start.2 = ((f32[32,64,128]{2,0,1:T(8,128)}), f32[32,64,128]{2,0,1:T(8,128)S(1)}, u32[]{:S(2)}, u32[]{:S(2)}) async-start(f32[32,64,128]{2,0,1:T(8,128)} %bitcast.102), calls=%async_computation.2 | async-start | bytes 2097152 | tf_op jit(solution)/shard_map/all_to_all | solution.py:60
  94.5 31.2 %all-to-all-start.4 = ((f32[32,32,256]{2,0,1:T(8,128)}), f32[32,32,256]{2,0,1:T(8,128)}, u32[]{:S(2)}, u32[]{:S(2)}) async-start(f32[32,32,256]{2,0,1:T(8,128)} %copy.93), calls=%async_computation.4 | async-start | bytes 2097152 | tf_op jit(solution)/shard_map/all_to_all | solution.py:87
  125.7 14.5 %copy-start.6 = (f32[32,8,1024]{2,0,1:T(8,128)S(1)}, f32[32,8,1024]{2,0,1:T(8,128)}, u32[]{:S(2)}) copy-start(f32[32,8,1024]{2,0,1:T(8,128)} %all_to_all.70) | copy-start | bytes 3145732
  132.8 35.5 %all-to-all-start.5 = ((f32[32,32,256]{2,1,0:T(8,128)}), f32[32,32,256]{2,1,0:T(8,128)S(1)}, u32[]{:S(2)}, u32[]{:S(2)}) async-start(f32[32,32,256]{2,1,0:T(8,128)} %fusion.15), calls=%async_computation.5 | async-start | bytes 2097152 | tf_op jit(solution)/shard_map/all_to_all | solution.py:89
  140.2 14.3 %copy-start = (f32[1024,1024]{1,0:T(8,128)S(1)}, f32[1024,1024]{1,0:T(8,128)}, u32[]{:S(2)}) copy-start(f32[1024,1024]{1,0:T(8,128)} %all-gather.2.cloned.1.call-done) | copy-start | bytes 12582916
  140.2 14.3 %copy-start.5 = (f32[32,8,1024]{2,0,1:T(8,128)S(1)}, f32[32,8,1024]{2,0,1:T(8,128)}, u32[]{:S(2)}) copy-start(f32[32,8,1024]{2,0,1:T(8,128)} %all_to_all.74) | copy-start | bytes 3145732
  147.4 19.1 %collective-permute-start = (f32[32,8,128]{2,0,1:T(8,128)}, f32[32,8,128]{2,0,1:T(8,128)}, u32[]{:S(2)}, u32[]{:S(2)}) collective-permute-start(f32[32,8,128]{2,0,1:T(8,128)} %get-tuple-element.21), channel_id=1, source_target_pairs={{0,1},{1,0},{2,3},{3,2},{4,5},{5,4},{6,7},{7,6},{8,9},{9,8},{10,11... | collective-permute-start | bytes 393224 | tf_op jit(solution)/shard_map/ppermute | solution.py:74
  147.6 27.3 %collective-permute-start.1 = (f32[32,8,128]{2,0,1:T(8,128)}, f32[32,8,128]{2,0,1:T(8,128)}, u32[]{:S(2)}, u32[]{:S(2)}) collective-permute-start(f32[32,8,128]{2,0,1:T(8,128)} %get-tuple-element.20), channel_id=1, source_target_pairs={{0,2},{1,3},{2,0},{3,1},{4,6},{5,7},{6,4},{7,5},{8,10},{9,11},{10,... | collective-permute-start | bytes 393224 | tf_op jit(solution)/shard_map/ppermute | solution.py:74
  147.6 31.6 %collective-permute-start.2 = (f32[32,8,128]{2,0,1:T(8,128)}, f32[32,8,128]{2,0,1:T(8,128)}, u32[]{:S(2)}, u32[]{:S(2)}) collective-permute-start(f32[32,8,128]{2,0,1:T(8,128)} %get-tuple-element.19), channel_id=1, source_target_pairs={{0,3},{1,2},{2,1},{3,0},{4,7},{5,6},{6,5},{7,4},{8,11},{9,10},{10,... | collective-permute-start | bytes 393224 | tf_op jit(solution)/shard_map/ppermute | solution.py:74
  150.9 29.9 %collective-permute-start.3 = (f32[32,8,128]{2,0,1:T(8,128)}, f32[32,8,128]{2,0,1:T(8,128)}, u32[]{:S(2)}, u32[]{:S(2)}) collective-permute-start(f32[32,8,128]{2,0,1:T(8,128)} %get-tuple-element.18), channel_id=1, source_target_pairs={{0,4},{1,5},{2,6},{3,7},{4,0},{5,1},{6,2},{7,3},{8,12},{9,13},{10,... | collective-permute-start | bytes 393224 | tf_op jit(solution)/shard_map/ppermute | solution.py:74
  151.2 31.4 %collective-permute-start.4 = (f32[32,8,128]{2,0,1:T(8,128)}, f32[32,8,128]{2,0,1:T(8,128)}, u32[]{:S(2)}, u32[]{:S(2)}) collective-permute-start(f32[32,8,128]{2,0,1:T(8,128)} %get-tuple-element.17), channel_id=1, source_target_pairs={{0,5},{1,4},{2,7},{3,6},{4,1},{5,0},{6,3},{7,2},{8,13},{9,12},{10,... | collective-permute-start | bytes 393224 | tf_op jit(solution)/shard_map/ppermute | solution.py:74
  166.5 1.0 copy-start.7
  167.5 16.7 %collective-permute-start.5 = (f32[32,8,128]{2,0,1:T(8,128)S(1)}, f32[32,8,128]{2,0,1:T(8,128)S(1)}, u32[]{:S(2)}, u32[]{:S(2)}) collective-permute-start(f32[32,8,128]{2,0,1:T(8,128)S(1)} %get-tuple-element.16), channel_id=1, source_target_pairs={{0,6},{1,7},{2,4},{3,5},{4,2},{5,3},{6,0},{7,1},{8,14},{9,15},{10,... | collective-permute-start | bytes 393224 | tf_op jit(solution)/shard_map/ppermute | solution.py:74
  168.3 44.0 %all-to-all-start.3 = ((f32[8,1,32768]{2,1,0:T(1,128)}), f32[8,1,32768]{2,1,0:T(1,128)S(1)}, u32[]{:S(2)}, u32[]{:S(2)}) async-start(f32[8,1,32768]{2,1,0:T(1,128)} %reshape.182), calls=%async_computation.3 | async-start | bytes 2097152 | tf_op jit(solution)/shard_map/all_to_all | solution.py:76
  174.9 32.6 %collective-permute-start.6 = (f32[32,8,128]{2,0,1:T(8,128)S(1)}, f32[32,8,128]{2,0,1:T(8,128)S(1)}, u32[]{:S(2)}, u32[]{:S(2)}) collective-permute-start(f32[32,8,128]{2,0,1:T(8,128)S(1)} %get-tuple-element.15), channel_id=1, source_target_pairs={{0,7},{1,6},{2,5},{3,4},{4,3},{5,2},{6,1},{7,0},{8,15},{9,14},{10,... | collective-permute-start | bytes 393224 | tf_op jit(solution)/shard_map/ppermute | solution.py:74
  215.9 6.5 %copy-start.3 = (f32[32,1,64,128]{3,2,1,0:T(8,128)S(1)}, f32[32,1,64,128]{3,2,1,0:T(8,128)}, u32[]{:S(2)}) copy-start(f32[32,1,64,128]{3,2,1,0:T(8,128)} %param.7) | copy-start | bytes 3145732
  215.9 6.5 %copy-start.8 = (pred[32,64]{1,0:T(8,128)(4,1)S(1)}, pred[32,64]{1,0:T(8,128)(4,1)}, u32[]{:S(2)}) copy-start(pred[32,64]{1,0:T(8,128)(4,1)} %add_compare_fusion.1) | copy-start | bytes 6148
Sparse Core Ops, SparseCore 0:
  25.4 49.3 all-gather.1
